TPU v7x, 256 devices: a whole 4x4x8 slice. The times are simulated.
256 devices in a mesh: rows: 64 (over x, z, core), cols: 4 (over y).
Axes of the slice: x: 4, y: 4, z: 8, core: 2. Of those that a mesh axis runs over, the one named last changes fastest.
Arguments:
- matrix: bfloat16 [131072, 1024], P('rows', 'cols'), as said below
- row_signs: int32 [131072], P('rows'), may hold values from 0 to 1
- sampled_rows: int32 [64, 2048], P('rows'), may hold values from 0 to 2047
- right_sides: float32 [8, 131072], P(None, 'rows'), may hold values from -6 to 6
Outputs:
- solution: float32 [8, 1024], P(None, 'cols')
- residual: float32 [8, 131072], P(None, 'rows')
Inputs may be any that keep to these rules, and one draw needn't show every extreme that they name: `matrix`: entries are at most 70 / sqrt(131072) in magnitude.
All inputs are finite; a program needn't handle non-finite values.
Results may differ from a plain program's by a relative error of at most 0.0013.
Values sent between devices are 32-bit elements; how exact they have to be, the bound alone decides.
No kernel may reach another device: no remote copies, remote signals or barrier semaphores. Data moves between devices by JAX's collectives and lax.ppermute only.
A program may use at most 64 MiB of HBM per device.

v0:
```python
import math
import jax
import jax.numpy as jnp
from jax import lax
from jax.sharding import PartitionSpec as P

SKETCH = 2048
ROUNDS = 2
highest = lax.Precision.HIGHEST


def split_up(shard, dim, size):
    before, after = (shard.shape[:dim], shard.shape[dim + 1 :])
    return jnp.moveaxis(shard.reshape(*before, size, -1, *after), dim, 0)


def sum_at_owner(shard, axis, dim):
    parts = split_up(shard, dim, lax.axis_size(axis))
    arrived = lax.all_to_all(parts, axis, split_axis=0, concat_axis=0, tiled=True)
    return arrived.sum(axis=0)


def sent_to_all(shard, axis):
    size = lax.axis_size(axis)
    return lax.all_to_all(
        jnp.broadcast_to(shard[None], (size, *shard.shape)), axis, 0, 0, tiled=True
    )


def laid_out(parts, dim):
    lengths = list(parts.shape[1:])
    lengths[dim] *= parts.shape[0]
    return jnp.moveaxis(parts, 0, dim).reshape(lengths)


def gathered_copies(shard, axis, dim):
    parts = sent_to_all(shard, axis)
    return laid_out(parts, dim)


def over_copies(shard, axis):
    everything = sent_to_all(shard, axis)
    return jnp.sum(everything, axis=0)


def in_one(arrays, axis):
    vector, at, finished = (jnp.concatenate([a.reshape(-1) for a in arrays]), 0, [])
    running = over_copies(vector, axis)
    for a in arrays:
        finished.append(running[at : at + a.size].reshape(a.shape))
        at += a.size
    return tuple(finished)


def sylvester(matrix_order):
    positions = jnp.arange(matrix_order, dtype=jnp.int32)
    common = jnp.bitwise_and(positions[:, None], positions[None, :])
    parity = jnp.zeros((matrix_order, matrix_order), jnp.int32)
    for bit_place in range(max(matrix_order.bit_length() - 1, 0)):
        parity = parity + jnp.bitwise_and(jnp.right_shift(common, bit_place), 1)
    return jnp.where(jnp.bitwise_and(parity, 1) == 0, 1.0, -1.0).astype(jnp.float32)


def transform(signed):
    row_count, col_count = signed.shape
    bit_count = row_count.bit_length() - 1
    outer_order = 2 ** (bit_count - bit_count // 2)
    inner_order = row_count // outer_order
    section_one = jnp.dot(
        sylvester(outer_order).astype(jnp.bfloat16),
        signed.reshape(outer_order, inner_order * col_count),
        preferred_element_type=jnp.float32,
    )
    second = jnp.einsum(
        "cd,adn->acn",
        sylvester(inner_order),
        section_one.reshape(outer_order, inner_order, col_count),
        precision=highest,
    )
    return second.reshape(row_count, col_count)


def solve_right(factor, vectors):
    return lax.linalg.triangular_solve(
        factor, vectors, left_side=False, lower=True, transpose_a=True
    )


def solve_left(factor, vectors):
    return lax.linalg.triangular_solve(
        factor, vectors, left_side=False, lower=True, transpose_a=False
    )


def local(matrix, row_signs, sampled_rows, right_sides):
    row_count, col_count = matrix.shape
    systems = right_sides.shape[0]
    flipped = (1 - 2 * row_signs).astype(jnp.bfloat16)
    signed = matrix * flipped[:, None]
    mixed_rows = transform(signed)
    picked = jnp.take(mixed_rows, sampled_rows[0], axis=0) * (1.0 / math.sqrt(SKETCH))
    sketch_piece = sum_at_owner(picked, "rows", 0)
    gram_block = lax.dot_general(
        gathered_copies(sketch_piece, "cols", 1),
        sketch_piece,
        (((0,), (0,)), ((), ())),
        precision=highest,
    )
    gram_band = sum_at_owner(gram_block, "rows", 0)
    gram_strip = gathered_copies(gram_band, "cols", 1)
    gram_matrix = lax.all_gather(gram_strip, "rows", axis=0, tiled=True)
    factor = jnp.linalg.cholesky(gram_matrix)
    col_start = lax.axis_index("cols") * col_count

    def forward(vectors):
        own_part = lax.dynamic_slice_in_dim(vectors, col_start, col_count, 1)
        local_part = lax.dot_general(
            own_part, matrix.astype(jnp.float32), (((1,), (1,)), ((), ())), precision=highest
        )
        return over_copies(local_part, "cols")

    def back_section(forward_rest):
        local_squares = jnp.sum(forward_rest * forward_rest, axis=1)
        local_part = jnp.dot(forward_rest, matrix.astype(jnp.float32), precision=highest)
        summed, total_squares = in_one((local_part, local_squares), "rows")
        beta_norm = jnp.sqrt(total_squares)
        summed = summed / beta_norm[:, None]
        left_unit = forward_rest / beta_norm[:, None]
        whole_vector = gathered_copies(summed, "cols", 1)
        return (beta_norm, left_unit, solve_right(factor, whole_vector))

    beta_norm, left_unit, back_rest = back_section(right_sides)
    alpha_norm = jnp.sqrt(jnp.sum(back_rest * back_rest, axis=1))
    right_unit = back_rest / alpha_norm[:, None]
    search = right_unit
    coeffs = jnp.zeros((systems, back_rest.shape[1]), jnp.float32)
    phibar = beta_norm
    rhobar = alpha_norm
    for iteration in range(ROUNDS):
        forward_rest = forward(solve_left(factor, right_unit)) - alpha_norm[:, None] * left_unit
        beta_norm, left_unit, back_rest = back_section(forward_rest)
        back_rest = back_rest - beta_norm[:, None] * right_unit
        alpha_norm = jnp.sqrt(jnp.sum(back_rest * back_rest, axis=1))
        right_unit = back_rest / alpha_norm[:, None]
        rho_total = jnp.sqrt(rhobar * rhobar + beta_norm * beta_norm)
        cosine = rhobar / rho_total
        sine_part = beta_norm / rho_total
        theta_term = sine_part * alpha_norm
        rhobar = -cosine * alpha_norm
        phi_term = cosine * phibar
        phibar = sine_part * phibar
        coeffs = coeffs + (phi_term / rho_total)[:, None] * search
        search = right_unit - (theta_term / rho_total)[:, None] * search
    full_solution = solve_left(factor, coeffs)
    residual = right_sides - forward(full_solution)
    solution = lax.dynamic_slice_in_dim(full_solution, col_start, col_count, 1)
    return (solution, residual)


def solution(mesh):
    in_specs = (P("rows", "cols"), P("rows"), P("rows", None), P(None, "rows"))
    out_specs = (P(None, "cols"), P(None, "rows"))
    return jax.shard_map(local, mesh=mesh, in_specs=in_specs, out_specs=out_specs, check_vma=False)
```

profile of v0, /device:TPU:1, one launch (start us, length us, event | category | flops | bytes accessed | tf_op | source)
XLA Modules:
  0.0 691.9 jit_solution(14446551683061149268)
XLA Ops:
  25.3 64.0 %all_to_all.63 = f32[64,32,256]{2,1,0:T(8,128)S(1)} all-to-all(f32[64,32,256]{2,1,0:T(8,128)S(1)} %select_multiply_fusion), channel_id=1, replica_groups=mesh['rows'=64,'cols'=4] {'rows'}, dimensions={0} | all-to-all | bytes 4194304 | tf_op jit(solution)/shard_map/all_to_all | solution.py:19
  99.6 35.6 %all_to_all.65 = f32[64,16,256]{2,1,0:T(8,128)S(1)} all-to-all(f32[64,16,256]{2,1,0:T(8,128)S(1)} %fusion.103), channel_id=1, replica_groups=mesh['rows'=64,'cols'=4] {'rows'}, dimensions={0} | all-to-all | bytes 2097152 | tf_op jit(solution)/shard_map/all_to_all | solution.py:19
  152.0 19.4 %all-to-all-done.4 = f32[64,1,2056]{2,1,0:T(1,128)S(1)} async-done(((f32[64,1,2056]{2,1,0:T(1,128)}), f32[64,1,2056]{2,1,0:T(1,128)S(1)}, u32[]{:S(2)}, u32[]{:S(2)}) %all-to-all-start.4) | async-done | bytes 526368 | tf_op jit(solution)/shard_map/all_to_all | solution.py:25
  175.7 43.4 %all-gather.2.cloned.1.call-done = f32[1024,1024]{1,0:T(8,128)} async-done(((f32[16,1024]{1,0:T(8,128)}), f32[1024,1024]{1,0:T(8,128)}) %all-gather.2.cloned.1.call-update) | async-done | bytes 4194320 | tf_op jit(solution)/shard_map/all_gather | solution.py:111
  231.0 11.7 %cholesky.223 = f32[128,128]{1,0:T(8,128)S(1)} custom-call(f32[128,128]{1,0:T(8,128)S(1)} %cholesky.580), custom_call_target="Cholesky" | custom-call | tf_op jit(solution)/shard_map/jit(cholesky)/cholesky | solution.py:112
  245.2 9.8 %custom-call.65 = f32[1,128,128]{1,2,0:T(8,128)S(1)} custom-call(f32[1,128,128]{2,1,0:T(8,128)S(1)} %get-tuple-element.83), custom_call_target="InvertDiagBlocksLowerTriangular" | custom-call | tf_op jit(solution)/shard_map/jit(cholesky)/cholesky | solution.py:112
  259.0 11.9 %cholesky.244 = f32[128,128]{1,0:T(8,128)S(1)} custom-call(f32[128,128]{1,0:T(8,128)S(1)} %cholesky.584), custom_call_target="Cholesky" | custom-call | tf_op jit(solution)/shard_map/jit(cholesky)/cholesky | solution.py:112
  271.5 9.8 %custom-call.66 = f32[1,128,128]{1,2,0:T(8,128)S(1)} custom-call(f32[1,128,128]{2,1,0:T(8,128)S(1)} %get-tuple-element.80), custom_call_target="InvertDiagBlocksLowerTriangular" | custom-call | tf_op jit(solution)/shard_map/jit(cholesky)/cholesky | solution.py:112
  284.7 11.7 %cholesky.468 = f32[128,128]{1,0:T(8,128)S(1)} custom-call(f32[128,128]{1,0:T(8,128)S(1)} %cholesky.589), custom_call_target="Cholesky" | custom-call | tf_op jit(solution)/shard_map/jit(cholesky)/cholesky | solution.py:112
  297.7 9.8 %custom-call.67 = f32[1,128,128]{1,2,0:T(8,128)S(1)} custom-call(f32[1,128,128]{2,1,0:T(8,128)S(1)} %get-tuple-element.77), custom_call_target="InvertDiagBlocksLowerTriangular" | custom-call | tf_op jit(solution)/shard_map/jit(cholesky)/cholesky | solution.py:112
  311.0 12.1 %cholesky.487 = f32[128,128]{1,0:T(8,128)S(1)} custom-call(f32[128,128]{1,0:T(8,128)S(1)} %cholesky.594), custom_call_target="Cholesky" | custom-call | tf_op jit(solution)/shard_map/jit(cholesky)/cholesky | solution.py:112
  324.4 9.8 %custom-call.68 = f32[1,128,128]{1,2,0:T(8,128)S(1)} custom-call(f32[1,128,128]{2,1,0:T(8,128)S(1)} %get-tuple-element.74), custom_call_target="InvertDiagBlocksLowerTriangular" | custom-call | tf_op jit(solution)/shard_map/jit(cholesky)/cholesky | solution.py:112
  337.7 11.7 %cholesky.506 = f32[128,128]{1,0:T(8,128)S(1)} custom-call(f32[128,128]{1,0:T(8,128)S(1)} %cholesky.599), custom_call_target="Cholesky" | custom-call | tf_op jit(solution)/shard_map/jit(cholesky)/cholesky | solution.py:112
  350.6 9.9 %custom-call.69 = f32[1,128,128]{1,2,0:T(8,128)S(1)} custom-call(f32[1,128,128]{2,1,0:T(8,128)S(1)} %get-tuple-element.71), custom_call_target="InvertDiagBlocksLowerTriangular" | custom-call | tf_op jit(solution)/shard_map/jit(cholesky)/cholesky | solution.py:112
  363.9 11.7 %cholesky.526 = f32[128,128]{1,0:T(8,128)S(1)} custom-call(f32[128,128]{1,0:T(8,128)S(1)} %cholesky.604), custom_call_target="Cholesky" | custom-call | tf_op jit(solution)/shard_map/jit(cholesky)/cholesky | solution.py:112
  376.9 9.8 %custom-call.70 = f32[1,128,128]{1,2,0:T(8,128)S(1)} custom-call(f32[1,128,128]{2,1,0:T(8,128)S(1)} %get-tuple-element.68), custom_call_target="InvertDiagBlocksLowerTriangular" | custom-call | tf_op jit(solution)/shard_map/jit(cholesky)/cholesky | solution.py:112
  389.7 11.9 %cholesky.546 = f32[128,128]{1,0:T(8,128)S(1)} custom-call(f32[128,128]{1,0:T(8,128)S(1)} %cholesky.609), custom_call_target="Cholesky" | custom-call | tf_op jit(solution)/shard_map/jit(cholesky)/cholesky | solution.py:112
  403.0 9.8 %custom-call.71 = f32[1,128,128]{1,2,0:T(8,128)S(1)} custom-call(f32[1,128,128]{2,1,0:T(8,128)S(1)} %get-tuple-element.65), custom_call_target="InvertDiagBlocksLowerTriangular" | custom-call | tf_op jit(solution)/shard_map/jit(cholesky)/cholesky | solution.py:112
  415.4 11.7 %cholesky.564 = f32[128,128]{1,0:T(8,128)S(1)} custom-call(f32[128,128]{1,0:T(8,128)S(1)} %convolution_subtract_fusion.6), custom_call_target="Cholesky" | custom-call | tf_op jit(solution)/shard_map/jit(cholesky)/cholesky | solution.py:112
  438.8 23.0 %while.10 = (s32[]{:T(128)}, f32[1024,1024]{1,0:T(8,128)}, s32[8,2]{0,1:T(2,128)S(1)}, f32[8,128,128]{2,1,0:T(8,128)S(1)}, s32[]{:T(128)}) while((s32[]{:T(128)}, f32[1024,1024]{1,0:T(8,128)}, s32[8,2]{0,1:T(2,128)S(1)}, f32[8,128,128]{2,1,0:T(8,128)S(1)}, s32[]{:T(128)}) %tuple.114), condition=%wide.while_cond, body=%wide.while_body.sunk | while | flops 2 | bytes 131181 | solution.py:84
  461.8 79.0 %custom-call.75 = f32[8,128,128]{1,2,0:T(8,128)S(1)} custom-call(f32[8,128,128]{2,1,0:T(8,128)S(1)} %get-tuple-element.38), custom_call_target="InvertDiagBlocksLowerTriangular" | custom-call | tf_op jit(solution)/shard_map/triangular_solve/custom-call.7 | solution.py:84
  562.8 10.0 %all_to_all.67 = f32[4,8,2048]{2,1,0:T(8,128)S(1)} all-to-all(f32[4,8,2048]{2,1,0:T(8,128)S(1)} %broadcast_in_dim.58), channel_id=1, replica_groups=mesh['rows'=64,'cols'=4] {'cols'}, dimensions={0} | all-to-all | bytes 524288 | tf_op jit(solution)/shard_map/all_to_all | solution.py:25
  573.9 25.1 %all_to_all.68 = f32[64,1,2056]{2,1,0:T(1,128)S(1)} all-to-all(f32[64,1,2056]{2,1,0:T(1,128)S(1)} %broadcast_in_dim.59), channel_id=1, replica_groups=mesh['rows'=64,'cols'=4] {'rows'}, dimensions={0} | all-to-all | bytes 1052672 | tf_op jit(solution)/shard_map/all_to_all | solution.py:25
  637.3 26.4 %all_to_all.71 = f32[64,1,2056]{2,1,0:T(1,128)S(1)} all-to-all(f32[64,1,2056]{2,1,0:T(1,128)S(1)} %broadcast_in_dim.62), channel_id=1, replica_groups=mesh['rows'=64,'cols'=4] {'rows'}, dimensions={0} | all-to-all | bytes 1052672 | tf_op jit(solution)/shard_map/all_to_all | solution.py:25
  (297 shorter events, 205.4 us)
Async XLA Ops:
  7.2 211.9 %all-gather.2.cloned.1.call-start = ((), (), s32[]{:S(2)}) async-start(), calls=%async_computation.12 | async-start | bytes 4259840 | tf_op jit(solution)/shard_map/all_gather | solution.py:111
  10.0 3.7 copy-start.4
  89.3 53.5 %copy-start = (bf16[2048,256]{1,0:T(8,128)(2,1)S(1)}, bf16[2048,256]{1,0:T(8,128)(2,1)}, u32[]{:S(2)}) copy-start(bf16[2048,256]{1,0:T(8,128)(2,1)} %param.8) | copy-start | bytes 3145732
  89.3 53.5 %copy-start.2 = (f32[8,2048]{1,0:T(8,128)S(1)}, f32[8,2048]{1,0:T(8,128)}, u32[]{:S(2)}) copy-start(f32[8,2048]{1,0:T(8,128)} %param.11) | copy-start | bytes 196612
  144.6 26.8 %all-to-all-start.4 = ((f32[64,1,2056]{2,1,0:T(1,128)}), f32[64,1,2056]{2,1,0:T(1,128)S(1)}, u32[]{:S(2)}, u32[]{:S(2)}) async-start(f32[64,1,2056]{2,1,0:T(1,128)} %broadcast_in_dim.56), calls=%async_computation.4 | async-start | bytes 1114112 | tf_op jit(solution)/shard_map/all_to_all | solution.py:25
  172.4 368.4 %all-to-all-start.5 = ((f32[4,8,256]{2,1,0:T(8,128)}), f32[4,8,256]{2,1,0:T(8,128)S(1)}, u32[]{:S(2)}, u32[]{:S(2)}) async-start(f32[4,8,256]{2,1,0:T(8,128)} %broadcast_in_dim.57), calls=%async_computation.5 | async-start | bytes 65536 | tf_op jit(solution)/shard_map/all_to_all | solution.py:25
  229.0 1.9 copy-start.1
  674.5 10.4 %copy-start.3 = (f32[8,256]{1,0:T(8,128)}, f32[8,256]{1,0:T(8,128)S(1)}, u32[]{:S(2)}) copy-start(f32[8,256]{1,0:T(8,128)S(1)} %constant_dynamic-slice_fusion.1) | copy-start | bytes 24580
Sparse Core Ops, SparseCore 0:
  142.9 76.1 all-gather.1
where the time goes:
time: 702 us; the launch traced here: 692 us
  other arithmetic  269 us (38%)
  blocking collectives  200 us (28%)
  matrix products  82.7 us (12%)
  waiting for transfers between devices  62.8 us (9%)
  local copies, waits for them, and re-layouts  46.3 us (7%)
  between operations  20.3 us (3%)
  starting transfers between devices  10.6 us (2%)
    another operation x30, other arithmetic, local(): factor = jnp.linalg.cholesky(gram_matrix)  172 us
    all_to_all x8, blocking collectives, sent_to_all(): lax.all_to_all(jnp.broadcast_to(shard[None], (size, *shard.shape)), axis,...  101 us
    all_to_all x2, blocking collectives, sum_at_owner(): lax.all_to_all(parts, axis, split_axis=0, concat_axis=0, tiled=True)  99.5 us
    another operation x4, other arithmetic, solve_right(): lax.linalg.triangular_solve(factor, vectors, left_side=False, lower=True,...  83.8 us
    all_gather x1, waiting for transfers between devices, local(): gram_matrix = lax.all_gather(gram_strip, 'rows', axis=0, tiled=True)  43.4 us
    another operation x45, matrix products, solve_left(): lax.linalg.triangular_solve(factor, vectors, left_side=False, lower=True,...  29.9 us
    another operation x14, matrix products, local(): factor = jnp.linalg.cholesky(gram_matrix)  23.1 us
    another operation x25, local copies, waits for them, and re-layouts, solve_right(): lax.linalg.triangular_solve(factor, vectors, left_side=False, lower=True,...  22.8 us
  transfers between devices with their start and end apart: 3, of which 2 were waited for; matrix products, arithmetic and copies ran while one was open for 46% of the time, Pallas kernels for 0%

commit v1 on v0

--- a/solution.py
+++ b/solution.py
@@ -108,7 +108,18 @@
     )
     gram_band = sum_at_owner(gram_block, "rows", 0)
     gram_strip = gathered_copies(gram_band, "cols", 1)
-    gram_matrix = lax.all_gather(gram_strip, "rows", axis=0, tiled=True)
+
+    def islands_work(point):
+        how_many = lax.axis_size("rows")
+        return lax.all_to_all(
+            jnp.tile(point, [how_many if nth == 0 else 1 for nth in range(point.ndim)]),
+            "rows",
+            split_axis=0,
+            concat_axis=0,
+            tiled=True,
+        )
+
+    gram_matrix = islands_work(gram_strip)
     factor = jnp.linalg.cholesky(gram_matrix)
     col_start = lax.axis_index("cols") * col_count
 

time: 702 us -> 751 us (1.070)
  waiting for transfers between devices: 62.8 us -> 146 us
  blocking collectives: 200 us -> 158 us
  starting transfers between devices: 10.6 us -> 27.6 us
  between operations: 20.3 us -> 7.06 us
    all_to_all x0 -> x2, waiting for transfers between devices: none -> 123 us  [the longest x1 95.4 us: islands_work(): lax.all_to_all(jnp.tile(point, [how_many if nth == 0 else 1 for nth in ra...]
    all_gather x1 -> x0, waiting for transfers between devices: 43.4 us -> none  [local(): gram_matrix = lax.all_gather(gram_strip, 'rows', axis=0, tiled=True)]
    all_to_all x2 -> x1, blocking collectives: 99.5 us -> 64 us  [sum_at_owner(): lax.all_to_all(parts, axis, split_axis=0, concat_axis=0, tiled=True)]
    all_to_all x0 -> x2, starting transfers between devices: none -> 13.7 us  [the longest x1 7.26 us: sum_at_owner(): lax.all_to_all(parts, axis, split_axis=0, concat_axis=0, tiled=True)]
    all_to_all x8 -> x7, blocking collectives: 101 us -> 94 us  [sent_to_all(): lax.all_to_all(jnp.broadcast_to(shard[None], (size, *shard.shape)), axis,...]
    all_to_all x2 -> x3, waiting for transfers between devices: 19.4 us -> 22.5 us  [sent_to_all(): lax.all_to_all(jnp.broadcast_to(shard[None], (size, *shard.shape)), axis,...]
  transfers between devices with their start and end apart: 3 -> 5, of which waited for: 2 -> 4; matrix products, arithmetic and copies ran while one was open for 46% -> 43% of each run, Pallas kernels for 0% -> 0%
where the time goes in v1:
time: 751 us; the launch traced here: 739 us
  other arithmetic  268 us (36%)
  blocking collectives  158 us (21%)
  waiting for transfers between devices  146 us (19%)
  matrix products  83.7 us (11%)
  local copies, waits for them, and re-layouts  48.9 us (7%)
  starting transfers between devices  27.6 us (4%)
    another operation x30, other arithmetic, local(): factor = jnp.linalg.cholesky(gram_matrix)  172 us
    all_to_all x1, waiting for transfers between devices, islands_work(): lax.all_to_all(jnp.tile(point, [how_many if nth == 0 else 1 for nth in ra...  95.4 us
    all_to_all x7, blocking collectives, sent_to_all(): lax.all_to_all(jnp.broadcast_to(shard[None], (size, *shard.shape)), axis,...  94 us
    another operation x4, other arithmetic, solve_right(): lax.linalg.triangular_solve(factor, vectors, left_side=False, lower=True,...  83.6 us
    all_to_all x1, blocking collectives, sum_at_owner(): lax.all_to_all(parts, axis, split_axis=0, concat_axis=0, tiled=True)  64 us
    another operation x45, matrix products, solve_left(): lax.linalg.triangular_solve(factor, vectors, left_side=False, lower=True,...  29.9 us
    all_to_all x1, waiting for transfers between devices, sum_at_owner(): lax.all_to_all(parts, axis, split_axis=0, concat_axis=0, tiled=True)  27.8 us
    another operation x14, matrix products, local(): factor = jnp.linalg.cholesky(gram_matrix)  23.1 us
  transfers between devices with their start and end apart: 5, of which 4 were waited for; matrix products, arithmetic and copies ran while one was open for 43% of the time, Pallas kernels for 0%

profile of v1, /device:TPU:1, one launch (start us, length us, event | category | flops | bytes accessed | tf_op | source)
XLA Modules:
  0.0 739.2 jit_solution(12663677279429568933)
XLA Ops:
  18.8 64.0 %all_to_all.72 = f32[64,32,256]{2,1,0:T(8,128)S(1)} all-to-all(f32[64,32,256]{2,1,0:T(8,128)S(1)} %select_multiply_fusion), channel_id=1, replica_groups=mesh['rows'=64,'cols'=4] {'rows'}, dimensions={0} | all-to-all | bytes 4194304 | tf_op jit(solution)/shard_map/all_to_all | solution.py:19
  102.0 27.8 %all-to-all-done.2 = f32[64,16,256]{2,1,0:T(8,128)S(1)} async-done(((f32[64,16,256]{2,1,0:T(8,128)}), f32[64,16,256]{2,1,0:T(8,128)S(1)}, u32[]{:S(2)}, u32[]{:S(2)}) %all-to-all-start.2) | async-done | bytes 1048608 | tf_op jit(solution)/shard_map/all_to_all | solution.py:19
  146.7 18.0 %all-to-all-done.5 = f32[64,1,2056]{2,1,0:T(1,128)S(1)} async-done(((f32[64,1,2056]{2,1,0:T(1,128)}), f32[64,1,2056]{2,1,0:T(1,128)S(1)}, u32[]{:S(2)}, u32[]{:S(2)}) %all-to-all-start.5) | async-done | bytes 526368 | tf_op jit(solution)/shard_map/all_to_all | solution.py:25
  174.2 95.4 %all-to-all-done.4 = f32[64,16,1024]{2,1,0:T(8,128)} async-done(((f32[64,16,1024]{2,1,0:T(8,128)}), f32[64,16,1024]{2,1,0:T(8,128)}, u32[]{:S(2)}, u32[]{:S(2)}) %all-to-all-start.4) | async-done | bytes 4194336 | tf_op jit(solution)/shard_map/all_to_all | solution.py:114
  285.5 11.7 %cholesky.223 = f32[128,128]{1,0:T(8,128)S(1)} custom-call(f32[128,128]{1,0:T(8,128)S(1)} %cholesky.580), custom_call_target="Cholesky" | custom-call | tf_op jit(solution)/shard_map/jit(cholesky)/cholesky | solution.py:123
  299.7 9.8 %custom-call.65 = f32[1,128,128]{1,2,0:T(8,128)S(1)} custom-call(f32[1,128,128]{2,1,0:T(8,128)S(1)} %get-tuple-element.83), custom_call_target="InvertDiagBlocksLowerTriangular" | custom-call | tf_op jit(solution)/shard_map/jit(cholesky)/cholesky | solution.py:123
  313.5 11.9 %cholesky.244 = f32[128,128]{1,0:T(8,128)S(1)} custom-call(f32[128,128]{1,0:T(8,128)S(1)} %cholesky.584), custom_call_target="Cholesky" | custom-call | tf_op jit(solution)/shard_map/jit(cholesky)/cholesky | solution.py:123
  326.0 9.8 %custom-call.66 = f32[1,128,128]{1,2,0:T(8,128)S(1)} custom-call(f32[1,128,128]{2,1,0:T(8,128)S(1)} %get-tuple-element.80), custom_call_target="InvertDiagBlocksLowerTriangular" | custom-call | tf_op jit(solution)/shard_map/jit(cholesky)/cholesky | solution.py:123
  339.1 11.7 %cholesky.468 = f32[128,128]{1,0:T(8,128)S(1)} custom-call(f32[128,128]{1,0:T(8,128)S(1)} %cholesky.589), custom_call_target="Cholesky" | custom-call | tf_op jit(solution)/shard_map/jit(cholesky)/cholesky | solution.py:123
  352.1 9.8 %custom-call.67 = f32[1,128,128]{1,2,0:T(8,128)S(1)} custom-call(f32[1,128,128]{2,1,0:T(8,128)S(1)} %get-tuple-element.77), custom_call_target="InvertDiagBlocksLowerTriangular" | custom-call | tf_op jit(solution)/shard_map/jit(cholesky)/cholesky | solution.py:123
  365.4 11.9 %cholesky.487 = f32[128,128]{1,0:T(8,128)S(1)} custom-call(f32[128,128]{1,0:T(8,128)S(1)} %cholesky.594), custom_call_target="Cholesky" | custom-call | tf_op jit(solution)/shard_map/jit(cholesky)/cholesky | solution.py:123
  378.6 9.8 %custom-call.68 = f32[1,128,128]{1,2,0:T(8,128)S(1)} custom-call(f32[1,128,128]{2,1,0:T(8,128)S(1)} %get-tuple-element.74), custom_call_target="InvertDiagBlocksLowerTriangular" | custom-call | tf_op jit(solution)/shard_map/jit(cholesky)/cholesky | solution.py:123
  391.9 11.7 %cholesky.506 = f32[128,128]{1,0:T(8,128)S(1)} custom-call(f32[128,128]{1,0:T(8,128)S(1)} %cholesky.599), custom_call_target="Cholesky" | custom-call | tf_op jit(solution)/shard_map/jit(cholesky)/cholesky | solution.py:123
  404.9 10.2 %custom-call.69 = f32[1,128,128]{1,2,0:T(8,128)S(1)} custom-call(f32[1,128,128]{2,1,0:T(8,128)S(1)} %get-tuple-element.71), custom_call_target="InvertDiagBlocksLowerTriangular" | custom-call | tf_op jit(solution)/shard_map/jit(cholesky)/cholesky | solution.py:123
  418.4 11.7 %cholesky.526 = f32[128,128]{1,0:T(8,128)S(1)} custom-call(f32[128,128]{1,0:T(8,128)S(1)} %cholesky.604), custom_call_target="Cholesky" | custom-call | tf_op jit(solution)/shard_map/jit(cholesky)/cholesky | solution.py:123
  431.4 9.8 %custom-call.70 = f32[1,128,128]{1,2,0:T(8,128)S(1)} custom-call(f32[1,128,128]{2,1,0:T(8,128)S(1)} %get-tuple-element.68), custom_call_target="InvertDiagBlocksLowerTriangular" | custom-call | tf_op jit(solution)/shard_map/jit(cholesky)/cholesky | solution.py:123
  444.2 11.9 %cholesky.546 = f32[128,128]{1,0:T(8,128)S(1)} custom-call(f32[128,128]{1,0:T(8,128)S(1)} %cholesky.609), custom_call_target="Cholesky" | custom-call | tf_op jit(solution)/shard_map/jit(cholesky)/cholesky | solution.py:123
  457.3 9.8 %custom-call.71 = f32[1,128,128]{1,2,0:T(8,128)S(1)} custom-call(f32[1,128,128]{2,1,0:T(8,128)S(1)} %get-tuple-element.65), custom_call_target="InvertDiagBlocksLowerTriangular" | custom-call | tf_op jit(solution)/shard_map/jit(cholesky)/cholesky | solution.py:123
  469.7 11.7 %cholesky.564 = f32[128,128]{1,0:T(8,128)S(1)} custom-call(f32[128,128]{1,0:T(8,128)S(1)} %convolution_subtract_fusion.6), custom_call_target="Cholesky" | custom-call | tf_op jit(solution)/shard_map/jit(cholesky)/cholesky | solution.py:123
  493.1 22.8 %while.10 = (s32[]{:T(128)}, f32[1024,1024]{1,0:T(8,128)}, s32[8,2]{0,1:T(2,128)S(1)}, f32[8,128,128]{2,1,0:T(8,128)S(1)}, s32[]{:T(128)}) while((s32[]{:T(128)}, f32[1024,1024]{1,0:T(8,128)}, s32[8,2]{0,1:T(2,128)S(1)}, f32[8,128,128]{2,1,0:T(8,128)S(1)}, s32[]{:T(128)}) %tuple.114), condition=%wide.while_cond, body=%wide.while_body.sunk | while | flops 2 | bytes 131181 | solution.py:84
  515.9 78.8 %custom-call.75 = f32[8,128,128]{1,2,0:T(8,128)S(1)} custom-call(f32[8,128,128]{2,1,0:T(8,128)S(1)} %get-tuple-element.38), custom_call_target="InvertDiagBlocksLowerTriangular" | custom-call | tf_op jit(solution)/shard_map/triangular_solve/custom-call.7 | solution.py:84
  616.7 9.7 %all_to_all.74 = f32[4,8,2048]{2,1,0:T(8,128)S(1)} all-to-all(f32[4,8,2048]{2,1,0:T(8,128)S(1)} %broadcast_in_dim.58), channel_id=1, replica_groups=mesh['rows'=64,'cols'=4] {'cols'}, dimensions={0} | all-to-all | bytes 524288 | tf_op jit(solution)/shard_map/all_to_all | solution.py:25
  627.4 25.4 %all_to_all.75 = f32[64,1,2056]{2,1,0:T(1,128)S(1)} all-to-all(f32[64,1,2056]{2,1,0:T(1,128)S(1)} %broadcast_in_dim.59), channel_id=1, replica_groups=mesh['rows'=64,'cols'=4] {'rows'}, dimensions={0} | all-to-all | bytes 1052672 | tf_op jit(solution)/shard_map/all_to_all | solution.py:25
  691.2 26.4 %all_to_all.78 = f32[64,1,2056]{2,1,0:T(1,128)S(1)} all-to-all(f32[64,1,2056]{2,1,0:T(1,128)S(1)} %broadcast_in_dim.62), channel_id=1, replica_groups=mesh['rows'=64,'cols'=4] {'rows'}, dimensions={0} | all-to-all | bytes 1052672 | tf_op jit(solution)/shard_map/all_to_all | solution.py:25
  (299 shorter events, 223.4 us)
Async XLA Ops:
  3.4 3.7 copy-start.4
  82.7 18.6 %copy-start = (bf16[2048,256]{1,0:T(8,128)(2,1)S(1)}, bf16[2048,256]{1,0:T(8,128)(2,1)}, u32[]{:S(2)}) copy-start(bf16[2048,256]{1,0:T(8,128)(2,1)} %param.8) | copy-start | bytes 3145732
  82.7 18.6 %copy-start.2 = (f32[8,2048]{1,0:T(8,128)S(1)}, f32[8,2048]{1,0:T(8,128)}, u32[]{:S(2)}) copy-start(f32[8,2048]{1,0:T(8,128)} %param.11) | copy-start | bytes 196612
  94.0 35.8 %all-to-all-start.2 = ((f32[64,16,256]{2,1,0:T(8,128)}), f32[64,16,256]{2,1,0:T(8,128)S(1)}, u32[]{:S(2)}, u32[]{:S(2)}) async-start(f32[64,16,256]{2,1,0:T(8,128)} %fusion.103), calls=%async_computation.2 | async-start | bytes 2097152 | tf_op jit(solution)/shard_map/all_to_all | solution.py:19
  130.5 7.7 %all-to-all-start.3 = ((f32[4,16,256]{2,1,0:T(8,128)}), f32[4,16,256]{2,1,0:T(8,128)S(1)}, u32[]{:S(2)}, u32[]{:S(2)}) async-start(f32[4,16,256]{2,1,0:T(8,128)} %broadcast_in_dim.55), calls=%async_computation.3 | async-start | bytes 131072 | tf_op jit(solution)/shard_map/all_to_all | solution.py:25
  139.4 25.4 %all-to-all-start.5 = ((f32[64,1,2056]{2,1,0:T(1,128)}), f32[64,1,2056]{2,1,0:T(1,128)S(1)}, u32[]{:S(2)}, u32[]{:S(2)}) async-start(f32[64,1,2056]{2,1,0:T(1,128)} %broadcast_in_dim.56), calls=%async_computation.5 | async-start | bytes 1114112 | tf_op jit(solution)/shard_map/all_to_all | solution.py:25
  167.2 102.3 %all-to-all-start.4 = ((f32[64,16,1024]{2,1,0:T(8,128)}), f32[64,16,1024]{2,1,0:T(8,128)}, u32[]{:S(2)}, u32[]{:S(2)}) async-start(f32[64,16,1024]{2,1,0:T(8,128)} %tile.9), calls=%async_computation.4 | async-start | bytes 8388608 | tf_op jit(solution)/shard_map/all_to_all | solution.py:114
  270.1 324.6 %all-to-all-start.6 = ((f32[4,8,256]{2,1,0:T(8,128)}), f32[4,8,256]{2,1,0:T(8,128)S(1)}, u32[]{:S(2)}, u32[]{:S(2)}) async-start(f32[4,8,256]{2,1,0:T(8,128)} %broadcast_in_dim.57), calls=%async_computation.6 | async-start | bytes 65536 | tf_op jit(solution)/shard_map/all_to_all | solution.py:25
  283.5 1.9 copy-start.1
  728.4 10.4 %copy-start.3 = (f32[8,256]{1,0:T(8,128)}, f32[8,256]{1,0:T(8,128)S(1)}, u32[]{:S(2)}) copy-start(f32[8,256]{1,0:T(8,128)S(1)} %constant_dynamic-slice_fusion.1) | copy-start | bytes 24580
